TPU v7x, 32 devices: a whole 2x2x4 slice. The times are simulated.
32 devices in a mesh: gx: 4 (over x, core), gy: 4 (over z), gz: 2 (over y).
Axes of the slice: x: 2, y: 2, z: 4, core: 2. Of those that a mesh axis runs over, the one named last changes fastest.
Arguments:
- deflation: bfloat16 [32, 16, 8, 3, 128], P('gx', 'gy', 'gz'), may hold values from -0.33 to 0.33
- material: int32 [32, 16, 8], P('gx', 'gy', 'gz'), may hold values from 0 to 15
- moduli: float32 [16], replicated, may hold values from 1 to 100
- stencil: float32 [27, 3, 3], replicated, may hold values from -0.6 to 0.6
Outputs:
- coarse: float32 [4, 4, 128, 2, 27, 128], P('gx', 'gy', 'gz')
All inputs are finite; a program needn't handle non-finite values.
Results may differ from a plain program's by a relative error of at most 0.005.
Values may be sent and summed in bfloat16 or wider, within the bound.
No kernel may reach another device: no remote copies, remote signals or barrier semaphores. Data moves between devices by JAX's collectives and lax.ppermute only.
A program may use at most 64 MiB of HBM per device.

v0:
```python
import functools

import jax
import jax.numpy as jnp
from jax import lax
from jax.experimental import pallas as pl
from jax.experimental.pallas import tpu as pltpu
from jax.sharding import PartitionSpec as P


VMEM = pltpu.VMEM
LANES = 128


def scale_kernel(
    moduli_hbm, material_hbm, vectors_hbm, stencil_hbm, out_ref, stencil_ref, moduli_ref, material_ref, vectors_ref, sems
):
    copies = [
        pltpu.make_async_copy(source, target, sems.at[i])
        for i, (source, target) in enumerate(
            (
                (moduli_hbm, moduli_ref),
                (material_hbm, material_ref),
                (vectors_hbm, vectors_ref),
                (stencil_hbm, stencil_ref),
            )
        )
    ]
    for copy in copies:
        copy.start()
    copies[0].wait()
    copies[1].wait()
    classes = moduli_ref.shape[0]
    cells_y, cells_z, cells_x = material_ref.shape
    parts = vectors_ref.shape[2]
    roots = []
    for y in range(cells_y):
        material = material_ref[y]
        modulus = jnp.zeros(material.shape, jnp.float32)
        for c in range(classes):
            modulus = jnp.where(material == c, moduli_ref[c], modulus)
        roots.append(jnp.sqrt(modulus))
    copies[2].wait()
    for x in range(cells_x):
        for y in range(cells_y):
            factor = jnp.broadcast_to(roots[y][:, x : x + 1], (cells_z, vectors_ref.shape[-1]))
            for a in range(parts):
                row = (y * parts + a) * cells_z
                value = vectors_ref[x, y, a].astype(jnp.float32) * factor
                out_ref[x, row : row + cells_z, :] = value.astype(jnp.bfloat16)
    copies[3].wait()


def weight_kernel(cells_z, stencil_ref, out_ref):
    _, rows, lanes = out_ref.shape
    parts, _, neighbours = stencil_ref.shape
    half = rows // 2
    block = parts * cells_z
    cells_y = half // block
    row = lax.broadcasted_iota(jnp.int32, (half, lanes), 0)
    lane = lax.broadcasted_iota(jnp.int32, (half, lanes), 1)
    slot = lane // block
    lane_y = jnp.where(slot < cells_y, slot, jnp.where(slot == cells_y, -1, cells_y))
    shift_y = jnp.where(slot < cells_y + 2, lane_y - row // block, 9)
    shift_z = lane % cells_z - row % cells_z
    pick_row = lax.broadcasted_iota(jnp.int32, (half, parts * neighbours), 0)
    pick_col = lax.broadcasted_iota(jnp.int32, (half, parts * neighbours), 1)
    pick_col = pick_col - neighbours * ((pick_row % block) // cells_z)
    spread = lax.broadcasted_iota(jnp.int32, (parts, lanes), 0) == (
        (lax.broadcasted_iota(jnp.int32, (parts, lanes), 1) % block) // cells_z
    )
    spread = spread.astype(jnp.float32).astype(jnp.bfloat16)
    wide = []
    for a in range(parts):
        exact = stencil_ref[a]
        high = exact.astype(jnp.bfloat16)
        low = (exact - high.astype(jnp.float32)).astype(jnp.bfloat16)
        wide.append(
            [
                lax.dot_general(piece, spread, (((0,), (0,)), ((), ())), preferred_element_type=jnp.float32)
                for piece in (high, low)
            ]
        )
    wide = [jnp.concatenate([w[h] for w in wide], axis=0).astype(jnp.bfloat16) for h in range(2)]
    wide = jnp.concatenate(wide, axis=1)
    for k in range(3):
        totals = [[jnp.zeros((half, lanes), jnp.float32) for _ in range(2)] for _ in range(3)]
        for dy in range(3):
            for dz in range(3):
                pick = (pick_col == 9 * k + 3 * dy + dz).astype(jnp.float32).astype(jnp.bfloat16)
                value = jnp.dot(pick, wide, preferred_element_type=jnp.float32)
                for oz in range(3):
                    here = (shift_y == dy - 1) & (shift_z == dz - 1 - (oz - 1) * cells_z)
                    for h in range(2):
                        totals[oz][h] = jnp.where(here, value[:, h * lanes : (h + 1) * lanes], totals[oz][h])
        for oz in range(3):
            for h in range(2):
                out_ref[3 * k + oz, h * half : (h + 1) * half, :] = totals[oz][h].astype(jnp.bfloat16)


def pairs_of(owners, place):
    if owners == 2:
        return [(u, v, place[v] - place[u] + 1) for u in range(2) for v in range(2)]
    return [(u, v, v - u + 1) for u in range(owners) for v in range(max(u - 1, 0), min(u + 2, owners))]


def image_kernel(share, places, rim_rows, weights_ref, *refs):
    owners = len(places(0))
    cells, (out_ref, turned_ref, image_ref) = refs[:owners], refs[owners:]
    cells_x, own_rows, _ = cells[0].shape
    rows = own_rows + rim_rows
    me = lax.axis_index("gz")
    first = me * share
    lane = lax.broadcasted_iota(jnp.int32, (share, LANES), 1)
    masks = [
        (lane >= own_rows) & (lane < own_rows + rim_rows // 2),
        lane < own_rows,
        (lane >= own_rows + rim_rows // 2) & (lane < rows),
    ]
    for u in range(owners):
        for x in range(cells_x):
            own = cells[u][x]
            turned_ref[x] = jnp.concatenate([own, own], axis=0).T
        for x in range(cells_x):
            image_ref[u, x * share : (x + 1) * share, :] = turned_ref[x, pl.ds(first, share), :]
    for pair, (u, v, oz) in enumerate(pairs_of(owners, places(me))):
        lhs = image_ref[u]
        products = [
            jnp.dot(lhs, weights_ref[3 * k + oz], preferred_element_type=jnp.float32) for k in range(3)
        ]
        for slot, x in enumerate([*range(cells_x), -1, cells_x]):
            total = None
            for k in range(3):
                source = x - (k - 1)
                if 0 <= source < cells_x:
                    term = products[k][source * share : (source + 1) * share, :]
                    total = term if total is None else total + term
            for oy, mask in enumerate(masks):
                tile = jnp.where(mask, total, 0.0).astype(jnp.bfloat16)
                out_ref[pair, slot, oy * share : (oy + 1) * share, :] = tile


def filled(pieces):
    pieces = list(pieces)
    missing = LANES - sum(p.shape[0] for p in pieces)
    return jnp.concatenate([*pieces, jnp.zeros((missing, pieces[0].shape[1]), pieces[0].dtype)], axis=0)


def putter(share, owners, out_ref):
    def put(n, u, value):
        out_ref[pl.ds(n * owners + u, share, stride=27 * owners), :] = value

    return put


def sides(share, put, tiles_ref, pair, u, oz, face_ref):
    slot = tiles_ref.shape[1] - 2
    for side in range(2):
        value = jnp.dot(
            tiles_ref[pair, slot + side], filled([face_ref[side]]), preferred_element_type=jnp.float32
        )
        for oy in range(3):
            put(18 * side + 3 * oy + oz, u, value[oy * share : (oy + 1) * share, :])


def middle_kernel(share, places, early, tiles_ref, *refs):
    owners = len(places(0))
    cells, rims, faces, out_ref = refs[:owners], refs[owners : 2 * owners], refs[2 * owners : -1], refs[-1]
    cells_x = cells[0].shape[0]
    place = places(lax.axis_index("gz"))
    put = putter(share, owners, out_ref)
    zero = jnp.zeros((share, out_ref.shape[1]), jnp.float32)
    for u in range(owners):
        if owners == 2:
            lost = [1 - place[1 - u] + place[u]]
        else:
            lost = [oz for oz in range(3) if not 0 <= u + oz - 1 < owners]
        for oz in lost:
            for n in range(0, 27, 3):
                put(n + oz, place[u], zero)
    for pair, (u, v, oz) in enumerate(pairs_of(owners, place)):
        if v in early:
            sides(share, put, tiles_ref, pair, place[u], oz, faces[early.index(v)])
        total = None
        for x in range(0, cells_x, 2):
            left = jnp.concatenate([tiles_ref[pair, x], tiles_ref[pair, x + 1]], axis=1)
            right = jnp.concatenate([filled([cells[v][i], rims[v][i]]) for i in (x, x + 1)], axis=0)
            term = jnp.dot(left, right, preferred_element_type=jnp.float32)
            total = term if total is None else total + term
        for oy in range(3):
            put(9 + 3 * oy + oz, place[u], total[oy * share : (oy + 1) * share, :])


def final_kernel(share, places, late, tiles_ref, *refs):
    faces, (_, whole_ref, out_ref, sem) = refs[: len(late)], refs[len(late) :]
    owners = len(places(0))
    place = places(lax.axis_index("gz"))
    put = putter(share, owners, whole_ref)
    for pair, (u, v, oz) in enumerate(pairs_of(owners, place)):
        if v in late:
            sides(share, put, tiles_ref, pair, place[u], oz, faces[late.index(v)])
    copy = pltpu.make_async_copy(whole_ref, out_ref, sem)
    copy.start()
    copy.wait()


def exchange(array, axes, flips, shift):
    sizes = [lax.axis_size(axis) for axis in axes]
    pairs = []
    for p in range(sizes[0]):
        to_p = (p + 1 if (p - shift) % 2 == 0 else p - 1) % sizes[0]
        if len(axes) == 1:
            pairs.append((p, to_p))
            continue
        for g in range(sizes[1]):
            pairs.append((p * sizes[1] + g, to_p * sizes[1] + (sizes[1] - 1 - g if flips else g)))
    return lax.ppermute(array, axes, pairs)


def sides_of(cells, rims):
    owners, cells_x = len(cells), cells[0].shape[0]
    wide, place = lax.axis_size("gx"), lax.axis_index("gx")

    def edge(v, x):
        return jnp.concatenate([cells[v][x], rims[v][x]], axis=0)

    if wide % 2 or owners != 2:
        left, right = halo(
            jnp.stack([edge(v, 0) for v in range(owners)]),
            jnp.stack([edge(v, cells_x - 1) for v in range(owners)]),
            "gx",
        )
    else:
        odd = place % 2 == 1
        across = jnp.where(odd, edge(0, cells_x - 1), edge(0, 0))
        far = exchange(across, ("gx", "gz"), True, 1)
        next_to = exchange(across, ("gx",), False, 1)
        beside = jnp.stack([jnp.where(odd, edge(v, 0), edge(v, cells_x - 1)) for v in range(owners)])
        beside = exchange(beside, ("gx",), False, 0)
        across = jnp.stack([next_to, far])
        left, right = jnp.where(odd, beside, across), jnp.where(odd, across, beside)
        zero = jnp.zeros_like(left)
        left, right = jnp.where(place == 0, zero, left), jnp.where(place == wide - 1, zero, right)
    return [jnp.stack([left[v], right[v]]) for v in range(owners)]


def in_hbm(array):
    return pltpu.with_memory_space_constraint(array, pltpu.HBM)


def cyclic(array, axis, step):
    peers = lax.axis_size(axis)
    return lax.ppermute(array, axis, [(i, (i + step) % peers) for i in range(peers)])


def halo(first, last, axis):
    peers, place = lax.axis_size(axis), lax.axis_index(axis)
    before = cyclic(last, axis, 1)
    after = cyclic(first, axis, -1)
    zero = jnp.zeros_like(before)
    return jnp.where(place == 0, zero, before), jnp.where(place == peers - 1, zero, after)


def columns(first, last):
    wide, peers = lax.axis_size("gx"), lax.axis_size("gy")
    if wide % 2:
        return halo(first, last, "gy")

    def target(p, q):
        if p % 2 == 0:
            return (p, q + 1) if q + 1 < peers else (p + 1, q)
        return (p, q - 1) if q > 0 else (p - 1, q)

    pairs = []
    for p in range(wide):
        for q in range(peers):
            to_p, to_q = target(p, q)
            pairs.append((p * peers + q, to_p * peers + to_q))
    place = lax.axis_index("gy")
    odd = lax.axis_index("gx") % 2 == 1
    ahead = lax.ppermute(jnp.where(odd, first, last), ("gx", "gy"), pairs)
    back = lax.ppermute(jnp.where(odd, last, first), ("gx", "gy"), [(t, f) for f, t in pairs])
    zero = jnp.zeros_like(ahead)
    before, after = jnp.where(odd, back, ahead), jnp.where(odd, ahead, back)
    return jnp.where(place == 0, zero, before), jnp.where(place == peers - 1, zero, after)


def line(array):
    owners = lax.axis_size("gz")
    if owners == 2:
        return [array, cyclic(array, "gz", 1)]
    gathered = lax.all_gather(array, "gz")
    return [gathered[v] for v in range(owners)]


def blocks(deflation, material, moduli, stencil):
    cells_x, cells_y, cells_z, parts, width = deflation.shape
    owners = lax.axis_size("gz")
    share = width // owners
    side = parts * cells_z
    own_rows = cells_y * side
    small = pltpu.CompilerParams(vmem_limit_bytes=16 << 20)
    vectors = jnp.transpose(deflation, (0, 1, 3, 2, 4))
    classes = jnp.transpose(material, (1, 2, 0))

    coupling = jnp.transpose(stencil, (1, 2, 0))
    scaled, coupling = pl.pallas_call(
        scale_kernel,
        out_shape=(
            jax.ShapeDtypeStruct((cells_x, own_rows, width), jnp.bfloat16),
            jax.ShapeDtypeStruct(coupling.shape, coupling.dtype),
        ),
        in_specs=[pl.BlockSpec(memory_space=pltpu.HBM)] * 4,
        out_specs=(pl.BlockSpec(memory_space=VMEM), pl.BlockSpec(memory_space=VMEM)),
        scratch_shapes=[
            pltpu.SMEM(moduli.shape, moduli.dtype),
            VMEM(classes.shape, classes.dtype),
            VMEM(vectors.shape, vectors.dtype),
            pltpu.SemaphoreType.DMA((4,)),
        ],
        compiler_params=small,
        name="scale",
    )(*(in_hbm(v) for v in (moduli, classes, vectors, coupling)))

    weights = pl.pallas_call(
        functools.partial(weight_kernel, cells_z),
        out_shape=jax.ShapeDtypeStruct((9, 2 * own_rows, LANES), jnp.bfloat16),
        in_specs=[pl.BlockSpec(memory_space=VMEM)],
        out_specs=pl.BlockSpec(memory_space=VMEM),
        compiler_params=small,
        name="weights",
    )(coupling)

    before, after = columns(scaled[:, :side], scaled[:, own_rows - side :])
    cells = line(scaled)
    rim = jnp.concatenate([before, after], axis=1)
    rims = line(rim)
    faces = sides_of(cells, rims)

    def places(me):
        return [me, 1 - me] if owners == 2 else list(range(owners))

    count = len(pairs_of(owners, places(0)))
    early = []
    late = [v for v in range(owners) if v not in early]
    in_vmem = pl.BlockSpec(memory_space=VMEM)
    tiles = pl.pallas_call(
        functools.partial(image_kernel, share, places, 2 * side),
        out_shape=jax.ShapeDtypeStruct((count, cells_x + 2, 3 * share, LANES), jnp.bfloat16),
        in_specs=[in_vmem] * (1 + owners),
        out_specs=in_vmem,
        scratch_shapes=[
            VMEM((cells_x, width, 2 * own_rows), jnp.bfloat16),
            VMEM((owners, cells_x * share, 2 * own_rows), jnp.bfloat16),
        ],
        compiler_params=small,
        name="image",
    )(weights, *cells)
    whole = jax.ShapeDtypeStruct((share * 27 * owners, width), jnp.float32)
    coarse = pl.pallas_call(
        functools.partial(middle_kernel, share, places, early),
        out_shape=pltpu.VMEM(whole.shape, whole.dtype),
        in_specs=[in_vmem] * (1 + 2 * owners + len(early)),
        out_specs=in_vmem,
        compiler_params=small,
        name="middle",
    )(tiles, *cells, *rims, *(faces[v] for v in early))
    _, coarse = pl.pallas_call(
        functools.partial(final_kernel, share, places, late),
        out_shape=(pltpu.VMEM(whole.shape, whole.dtype), whole),
        in_specs=[in_vmem] * (2 + len(late)),
        out_specs=(in_vmem, pl.BlockSpec(memory_space=pltpu.HBM)),
        scratch_shapes=[pltpu.SemaphoreType.DMA],
        input_output_aliases={1 + len(late): 0},
        compiler_params=small,
        name="final",
    )(tiles, *(faces[v] for v in late), coarse)
    coarse = coarse.reshape(share, 27, owners, width)
    return jnp.transpose(coarse, (0, 2, 1, 3)).reshape(1, 1, share, owners, 27, width)


def solution(mesh):
    in_specs = (P("gx", "gy", "gz", None, None), P("gx", "gy", "gz"), P(), P())
    out_specs = P("gx", "gy", "gz", None, None, None)
    return jax.shard_map(blocks, mesh=mesh, in_specs=in_specs, out_specs=out_specs, check_vma=False)
```

profile of v0, /device:TPU:0, one launch (start us, length us, event | category | flops | bytes accessed | tf_op | source)
XLA Modules:
  0.0 19.0 jit_solution(12306481639171232948)
XLA Ops:
  0.0 1.1 %scale.1 = (bf16[8,48,128]{2,1,0:T(8,128)(2,1)S(1)}, f32[3,3,27]{2,1,0:T(4,128)S(1)}) custom-call(f32[16]{0:T(128)} %moduli_hbm.1, s32[4,4,8]{2,1,0:T(4,128)} %bitcast.21, bf16[8,4,3,4,128]{4,3,2,1,0:T(4,128)(2,1)} %bitcast.16, f32[3,3,27]{2,1,0:T(4,128)} %bitcast.22), custom_call_target="tpu_custom_call" | custom-call | tf_op jit(solution)/shard_map/scale/pallas_call | solution.py:307
  1.1 3.1 %collective-permute-start = (bf16[8,48,128]{2,1,0:T(8,128)(2,1)S(1)}, bf16[8,48,128]{2,1,0:T(8,128)(2,1)S(1)}, u32[]{:S(2)}, u32[]{:S(2)}) collective-permute-start(bf16[8,48,128]{2,1,0:T(8,128)(2,1)S(1)} %get-tuple-element.9.refs_0_), channel_id=1, source_target_pairs={{0,1},{1,0},{2,3},{3,2},{4,5},{5,4},{6,7},{7,6},{8,9},{9,8},{10,11... | collective-permute-start | bytes 294920 | tf_op jit(solution)/shard_map/ppermute | solution.py:253
  4.1 0.0 collective-permute-start.1
  4.2 2.0 %collective-permute-start.2 = (bf16[8,12,128]{2,1,0:T(8,128)(2,1)S(1)}, bf16[8,12,128]{2,1,0:T(8,128)(2,1)S(1)}, u32[]{:S(2)}, u32[]{:S(2)}) collective-permute-start(bf16[8,12,128]{2,1,0:T(8,128)(2,1)S(1)} %get-tuple-element.18), channel_id=1, source_target_pairs={{0,2},{2,4},{4,6},{6,14},{8,0},{10,8},{12,10},{14,12},{16,18},{18,... | collective-permute-start | bytes 73736 | tf_op jit(solution)/shard_map/ppermute | solution.py:281
  6.2 2.1 %collective-permute-done.1 = bf16[8,12,128]{2,1,0:T(8,128)(2,1)S(1)} collective-permute-done((bf16[8,12,128]{2,1,0:T(8,128)(2,1)S(1)}, bf16[8,12,128]{2,1,0:T(8,128)(2,1)S(1)}, u32[]{:S(2)}, u32[]{:S(2)}) %collective-permute-start.1) | collective-permute-done | bytes 24608 | tf_op jit(solution)/shard_map/ppermute | solution.py:282
  8.3 0.0 collective-permute-done.2
  8.4 0.1 collective-permute-start.3
  8.5 4.1 %collective-permute-done.3.refs_3_ = bf16[8,24,128]{2,1,0:T(8,128)(2,1)S(1)} collective-permute-done((bf16[8,24,128]{2,1,0:T(8,128)(2,1)S(1)}, bf16[8,24,128]{2,1,0:T(8,128)(2,1)S(1)}, u32[]{:S(2)}, u32[]{:S(2)}) %collective-permute-start.3) | collective-permute-done | bytes 49184 | tf_op jit(solution)/shard_map/ppermute | solution.py:253
  12.5 0.0 collective-permute-done.refs_1_
  12.6 0.1 collective-permute-start.4
  12.7 1.6 %collective-permute-start.6 = (bf16[72,128]{1,0:T(8,128)(2,1)S(1)}, bf16[72,128]{1,0:T(8,128)(2,1)S(1)}, u32[]{:S(2)}, u32[]{:S(2)}) collective-permute-start(bf16[72,128]{1,0:T(8,128)(2,1)S(1)} %maximum_select_fusion.2), channel_id=1, source_target_pairs={{0,25},{1,24},{8,17},{9,16},{16,9},{17,8},{24,1},{25,0},{2,27},{3,... | collective-permute-start | bytes 55304 | tf_op jit(solution)/shard_map/ppermute | solution.py:217
  14.3 0.1 collective-permute-start.5
  14.4 0.5 %weights.1.weights_ref = bf16[9,96,128]{2,1,0:T(8,128)(2,1)S(1)} custom-call(f32[3,3,27]{2,1,0:T(4,128)S(1)} %get-tuple-element.8.stencil_ref), custom_call_target="tpu_custom_call" | custom-call | tf_op jit(solution)/shard_map/weights/pallas_call | solution.py:325
  14.9 0.8 %image.1.tiles_ref = bf16[4,10,192,128]{3,2,1,0:T(8,128)(2,1)S(1)} custom-call(bf16[9,96,128]{2,1,0:T(8,128)(2,1)S(1)} %weights.1.weights_ref, bf16[8,48,128]{2,1,0:T(8,128)(2,1)S(1)} %get-tuple-element.9.refs_0_, bf16[8,48,128]{2,1,0:T(8,128)(2,1)S(1)} %collective-permute-done.refs_1_), custom_call_target="tpu_custom_call" | custom-call | tf_op jit(solution)/shard_map/image/pallas_call | solution.py:347
  15.8 0.6 %middle.1.refs_2_ = f32[3456,128]{1,0:T(8,128)S(1)} custom-call(bf16[4,10,192,128]{3,2,1,0:T(8,128)(2,1)S(1)} %image.1.tiles_ref, bf16[8,48,128]{2,1,0:T(8,128)(2,1)S(1)} %get-tuple-element.9.refs_0_, bf16[8,48,128]{2,1,0:T(8,128)(2,1)S(1)} %collective-permute-done.refs_1_, bf16[8,24,128]{2,1,0:T(8,128)(2,1)S(1)} %pad_maximum_fusion.refs_2_, ...), custom_call_target="tpu_custom_call" | custom-call | tf_op jit(solution)/shard_map/middle/pallas_call | solution.py:360
  16.3 0.5 %collective-permute-done.6 = bf16[72,128]{1,0:T(8,128)(2,1)S(1)} collective-permute-done((bf16[72,128]{1,0:T(8,128)(2,1)S(1)}, bf16[72,128]{1,0:T(8,128)(2,1)S(1)}, u32[]{:S(2)}, u32[]{:S(2)}) %collective-permute-start.6) | collective-permute-done | bytes 18464 | tf_op jit(solution)/shard_map/ppermute | solution.py:217
  16.8 0.6 %collective-permute-done.5 = bf16[72,128]{1,0:T(8,128)(2,1)S(1)} collective-permute-done((bf16[72,128]{1,0:T(8,128)(2,1)S(1)}, bf16[72,128]{1,0:T(8,128)(2,1)S(1)}, u32[]{:S(2)}, u32[]{:S(2)}) %collective-permute-start.5) | collective-permute-done | bytes 18464 | tf_op jit(solution)/shard_map/ppermute | solution.py:217
  17.4 0.0 collective-permute-done.4
  17.5 1.5 %final.1 = (f32[3456,128]{1,0:T(8,128)S(1)}, f32[3456,128]{1,0:T(8,128)}) custom-call(bf16[4,10,192,128]{3,2,1,0:T(8,128)(2,1)S(1)} %image.1.tiles_ref, bf16[2,72,128]{2,1,0:T(8,128)(2,1)S(1)} %pad_maximum_fusion.3.refs_0_, bf16[2,72,128]{2,1,0:T(8,128)(2,1)S(1)} %pad_maximum_fusion.4.refs_1_, ...), custom_call_target="tpu_custom_call", output_to_operand_aliasing={{0}: (3, {})} | custom-call | tf_op jit(solution)/shard_map/final/pallas_call | solution.py:368
  (15 shorter events, 0.1 us)
Async XLA Ops:
  1.1 11.4 %collective-permute-start = (bf16[8,48,128]{2,1,0:T(8,128)(2,1)S(1)}, bf16[8,48,128]{2,1,0:T(8,128)(2,1)S(1)}, u32[]{:S(2)}, u32[]{:S(2)}) collective-permute-start(bf16[8,48,128]{2,1,0:T(8,128)(2,1)S(1)} %get-tuple-element.9.refs_0_), channel_id=1, source_target_pairs={{0,1},{1,0},{2,3},{3,2},{4,5},{5,4},{6,7},{7,6},{8,9},{9,8},{10,11... | collective-permute-start | bytes 294920 | tf_op jit(solution)/shard_map/ppermute | solution.py:253
  4.1 4.2 %collective-permute-start.1 = (bf16[8,12,128]{2,1,0:T(8,128)(2,1)S(1)}, bf16[8,12,128]{2,1,0:T(8,128)(2,1)S(1)}, u32[]{:S(2)}, u32[]{:S(2)}) collective-permute-start(bf16[8,12,128]{2,1,0:T(8,128)(2,1)S(1)} %get-tuple-element.17), channel_id=1, source_target_pairs={{2,0},{4,2},{6,4},{14,6},{0,8},{8,10},{10,12},{12,14},{18,16},{20,... | collective-permute-start | bytes 73736 | tf_op jit(solution)/shard_map/ppermute | solution.py:282
  4.2 4.1 %collective-permute-start.2 = (bf16[8,12,128]{2,1,0:T(8,128)(2,1)S(1)}, bf16[8,12,128]{2,1,0:T(8,128)(2,1)S(1)}, u32[]{:S(2)}, u32[]{:S(2)}) collective-permute-start(bf16[8,12,128]{2,1,0:T(8,128)(2,1)S(1)} %get-tuple-element.18), channel_id=1, source_target_pairs={{0,2},{2,4},{4,6},{6,14},{8,0},{10,8},{12,10},{14,12},{16,18},{18,... | collective-permute-start | bytes 73736 | tf_op jit(solution)/shard_map/ppermute | solution.py:281
  8.4 4.2 %collective-permute-start.3 = (bf16[8,24,128]{2,1,0:T(8,128)(2,1)S(1)}, bf16[8,24,128]{2,1,0:T(8,128)(2,1)S(1)}, u32[]{:S(2)}, u32[]{:S(2)}) collective-permute-start(bf16[8,24,128]{2,1,0:T(8,128)(2,1)S(1)} %pad_maximum_fusion.refs_2_), channel_id=1, source_target_pairs={{0,1},{1,0},{2,3},{3,2},{4,5},{5,4},{6,7},{7,6},{8,9},{9,8},{10,11... | collective-permute-start | bytes 147464 | tf_op jit(solution)/shard_map/ppermute | solution.py:253
  12.6 4.9 %collective-permute-start.4 = (bf16[2,72,128]{2,1,0:T(8,128)(2,1)S(1)}, bf16[2,72,128]{2,1,0:T(8,128)(2,1)S(1)}, u32[]{:S(2)}, u32[]{:S(2)}) collective-permute-start(bf16[2,72,128]{2,1,0:T(8,128)(2,1)S(1)} %pad_maximum_fusion.1), channel_id=1, source_target_pairs={{0,8},{8,0},{16,24},{24,16},{1,9},{9,1},{17,25},{25,17},{2,10},{10... | collective-permute-start | bytes 110600 | tf_op jit(solution)/shard_map/ppermute | solution.py:217
  12.7 4.2 %collective-permute-start.6 = (bf16[72,128]{1,0:T(8,128)(2,1)S(1)}, bf16[72,128]{1,0:T(8,128)(2,1)S(1)}, u32[]{:S(2)}, u32[]{:S(2)}) collective-permute-start(bf16[72,128]{1,0:T(8,128)(2,1)S(1)} %maximum_select_fusion.2), channel_id=1, source_target_pairs={{0,25},{1,24},{8,17},{9,16},{16,9},{17,8},{24,1},{25,0},{2,27},{3,... | collective-permute-start | bytes 55304 | tf_op jit(solution)/shard_map/ppermute | solution.py:217
  14.3 3.2 %collective-permute-start.5 = (bf16[72,128]{1,0:T(8,128)(2,1)S(1)}, bf16[72,128]{1,0:T(8,128)(2,1)S(1)}, u32[]{:S(2)}, u32[]{:S(2)}) collective-permute-start(bf16[72,128]{1,0:T(8,128)(2,1)S(1)} %maximum_select_fusion.2), channel_id=1, source_target_pairs={{0,24},{8,16},{16,8},{24,0},{1,25},{9,17},{17,9},{25,1},{2,26},{10... | collective-permute-start | bytes 55304 | tf_op jit(solution)/shard_map/ppermute | solution.py:217
where the time goes:
time: 19.1 us; the launch traced here: 19 us
  waiting for transfers between devices  7.29 us (38%)
  starting transfers between devices  6.97 us (36%)
  Pallas kernels  4.43 us (23%)
    ppermute x2, waiting for transfers between devices, cyclic(): lax.ppermute(array, axis, [(i, (i + step) % peers) for i in range(peers)])  4.06 us
    ppermute x2, starting transfers between devices, cyclic(): lax.ppermute(array, axis, [(i, (i + step) % peers) for i in range(peers)])  3.13 us
    ppermute x1, waiting for transfers between devices, columns(): lax.ppermute(jnp.where(odd, last, first), ('gx', 'gy'), [(t, f) for f, t...  2.11 us
    ppermute x1, starting transfers between devices, columns(): ahead = lax.ppermute(jnp.where(odd, first, last), ('gx', 'gy'), pairs)  2.01 us
    ppermute x3, starting transfers between devices, exchange(): return lax.ppermute(array, axes, pairs)  1.8 us
    pallas_call x1, Pallas kernels, blocks(): pl.pallas_call(functools.partial(final_kernel, share, places, late), out_...  1.46 us
    ppermute x3, waiting for transfers between devices, exchange(): return lax.ppermute(array, axes, pairs)  1.11 us
    pallas_call x1, Pallas kernels, blocks(): pl.pallas_call(scale_kernel, out_shape=(jax.ShapeDtypeStruct((cells_x, ow...  1.06 us
  transfers between devices with their start and end apart: 7, of which 4 were waited for; matrix products, arithmetic and copies ran while one was open for 0% of the time, Pallas kernels for 10%

commit v1 on v0

--- a/solution.py
+++ b/solution.py
@@ -10,6 +10,8 @@
 
 VMEM = pltpu.VMEM
 LANES = 128
+ROUNDS = 2
+PIECES = 4
 
 
 def scale_kernel(
@@ -21,10 +23,15 @@
             (
                 (moduli_hbm, moduli_ref),
                 (material_hbm, material_ref),
-                (vectors_hbm, vectors_ref),
                 (stencil_hbm, stencil_ref),
             )
         )
+    ]
+    parts_x = vectors_ref.shape[0] // PIECES
+    pieces = [pl.ds(i * parts_x, parts_x) for i in range(PIECES)]
+    copies[2:2] = [
+        pltpu.make_async_copy(vectors_hbm.at[piece], vectors_ref.at[piece], sems.at[3 + i])
+        for i, piece in enumerate(pieces)
     ]
     for copy in copies:
         copy.start()
@@ -40,7 +47,8 @@
         for c in range(classes):
             modulus = jnp.where(material == c, moduli_ref[c], modulus)
         roots.append(jnp.sqrt(modulus))
-    copies[2].wait()
+    for copy in copies[2:-1]:
+        copy.wait()
     for x in range(cells_x):
         for y in range(cells_y):
             factor = jnp.broadcast_to(roots[y][:, x : x + 1], (cells_z, vectors_ref.shape[-1]))
@@ -48,7 +56,7 @@
                 row = (y * parts + a) * cells_z
                 value = vectors_ref[x, y, a].astype(jnp.float32) * factor
                 out_ref[x, row : row + cells_z, :] = value.astype(jnp.bfloat16)
-    copies[3].wait()
+    copies[-1].wait()
 
 
 def weight_kernel(cells_z, stencil_ref, out_ref):
@@ -146,26 +154,28 @@
     return jnp.concatenate([*pieces, jnp.zeros((missing, pieces[0].shape[1]), pieces[0].dtype)], axis=0)
 
 
-def putter(share, owners, out_ref):
+def putter(share, owners, out_ref, start=0):
     def put(n, u, value):
-        out_ref[pl.ds(n * owners + u, share, stride=27 * owners), :] = value
+        out_ref[pl.ds((start * 27 + n) * owners + u, share, stride=27 * owners), :] = value
 
     return put
 
 
-def sides(share, put, tiles_ref, pair, u, oz, face_ref):
+def sides(share, put, tiles_ref, pair, u, oz, face_ref, start, size):
     slot = tiles_ref.shape[1] - 2
     for side in range(2):
-        value = jnp.dot(
-            tiles_ref[pair, slot + side], filled([face_ref[side]]), preferred_element_type=jnp.float32
+        left = jnp.concatenate(
+            [tiles_ref[pair, slot + side, oy * share + start : oy * share + start + size, :] for oy in range(3)],
+            axis=0,
         )
+        value = jnp.dot(left, filled([face_ref[side]]), preferred_element_type=jnp.float32)
         for oy in range(3):
-            put(18 * side + 3 * oy + oz, u, value[oy * share : (oy + 1) * share, :])
-
-
-def middle_kernel(share, places, early, tiles_ref, *refs):
+            put(18 * side + 3 * oy + oz, u, value[oy * size : (oy + 1) * size, :])
+
+
+def middle_kernel(share, places, tiles_ref, *refs):
     owners = len(places(0))
-    cells, rims, faces, out_ref = refs[:owners], refs[owners : 2 * owners], refs[2 * owners : -1], refs[-1]
+    cells, rims, out_ref = refs[:owners], refs[owners : 2 * owners], refs[-1]
     cells_x = cells[0].shape[0]
     place = places(lax.axis_index("gz"))
     put = putter(share, owners, out_ref)
@@ -179,8 +189,6 @@
             for n in range(0, 27, 3):
                 put(n + oz, place[u], zero)
     for pair, (u, v, oz) in enumerate(pairs_of(owners, place)):
-        if v in early:
-            sides(share, put, tiles_ref, pair, place[u], oz, faces[early.index(v)])
         total = None
         for x in range(0, cells_x, 2):
             left = jnp.concatenate([tiles_ref[pair, x], tiles_ref[pair, x + 1]], axis=1)
@@ -195,13 +203,18 @@
     faces, (_, whole_ref, out_ref, sem) = refs[: len(late)], refs[len(late) :]
     owners = len(places(0))
     place = places(lax.axis_index("gz"))
-    put = putter(share, owners, whole_ref)
-    for pair, (u, v, oz) in enumerate(pairs_of(owners, place)):
-        if v in late:
-            sides(share, put, tiles_ref, pair, place[u], oz, faces[late.index(v)])
-    copy = pltpu.make_async_copy(whole_ref, out_ref, sem)
-    copy.start()
-    copy.wait()
+    rounds = sem.shape[0]
+    size = share // rounds
+    copies = []
+    for i in range(rounds):
+        put = putter(size, owners, whole_ref, i * size)
+        for pair, (u, v, oz) in enumerate(pairs_of(owners, place)):
+            sides(share, put, tiles_ref, pair, place[u], oz, faces[late.index(v)], i * size, size)
+        span = pl.ds(i * size * 27 * owners, size * 27 * owners)
+        copies.append(pltpu.make_async_copy(whole_ref.at[span], out_ref.at[span], sem.at[i]))
+        copies[-1].start()
+    for copy in copies:
+        copy.wait()
 
 
 def exchange(array, axes, flips, shift):
@@ -316,7 +329,7 @@
             pltpu.SMEM(moduli.shape, moduli.dtype),
             VMEM(classes.shape, classes.dtype),
             VMEM(vectors.shape, vectors.dtype),
-            pltpu.SemaphoreType.DMA((4,)),
+            pltpu.SemaphoreType.DMA((3 + PIECES,)),
         ],
         compiler_params=small,
         name="scale",
@@ -358,7 +371,7 @@
     )(weights, *cells)
     whole = jax.ShapeDtypeStruct((share * 27 * owners, width), jnp.float32)
     coarse = pl.pallas_call(
-        functools.partial(middle_kernel, share, places, early),
+        functools.partial(middle_kernel, share, places),
         out_shape=pltpu.VMEM(whole.shape, whole.dtype),
         in_specs=[in_vmem] * (1 + 2 * owners + len(early)),
         out_specs=in_vmem,
@@ -370,7 +383,7 @@
         out_shape=(pltpu.VMEM(whole.shape, whole.dtype), whole),
         in_specs=[in_vmem] * (2 + len(late)),
         out_specs=(in_vmem, pl.BlockSpec(memory_space=pltpu.HBM)),
-        scratch_shapes=[pltpu.SemaphoreType.DMA],
+        scratch_shapes=[pltpu.SemaphoreType.DMA((ROUNDS,))],
         input_output_aliases={1 + len(late): 0},
         compiler_params=small,
         name="final",

time: 19.1 us -> 19 us (level)
  no operation moved by 1% of the time
where the time goes in v1:
time: 19 us; the launch traced here: 18.9 us
  waiting for transfers between devices  7.28 us (38%)
  starting transfers between devices  6.97 us (37%)
  Pallas kernels  4.32 us (23%)
    ppermute x2, waiting for transfers between devices, cyclic(): lax.ppermute(array, axis, [(i, (i + step) % peers) for i in range(peers)])  4.06 us
    ppermute x2, starting transfers between devices, cyclic(): lax.ppermute(array, axis, [(i, (i + step) % peers) for i in range(peers)])  3.13 us
    ppermute x1, waiting for transfers between devices, columns(): lax.ppermute(jnp.where(odd, last, first), ('gx', 'gy'), [(t, f) for f, t...  2.11 us
    ppermute x1, starting transfers between devices, columns(): ahead = lax.ppermute(jnp.where(odd, first, last), ('gx', 'gy'), pairs)  2.01 us
    ppermute x3, starting transfers between devices, exchange(): return lax.ppermute(array, axes, pairs)  1.8 us
    pallas_call x1, Pallas kernels, blocks(): pl.pallas_call(functools.partial(final_kernel, share, places, late), out_...  1.41 us
    ppermute x3, waiting for transfers between devices, exchange(): return lax.ppermute(array, axes, pairs)  1.11 us
    pallas_call x1, Pallas kernels, blocks(): pl.pallas_call(scale_kernel, out_shape=(jax.ShapeDtypeStruct((cells_x, ow...  0.98 us
  transfers between devices with their start and end apart: 7, of which 4 were waited for; matrix products, arithmetic and copies ran while one was open for 0% of the time, Pallas kernels for 10%

profile of v1, /device:TPU:0, one launch (start us, length us, event | category | flops | bytes accessed | tf_op | source)
XLA Modules:
  0.0 18.9 jit_solution(9179105246770518123)
XLA Ops:
  0.0 1.0 %scale.1 = (bf16[8,48,128]{2,1,0:T(8,128)(2,1)S(1)}, f32[3,3,27]{2,1,0:T(4,128)S(1)}) custom-call(f32[16]{0:T(128)} %moduli_hbm.1, s32[4,4,8]{2,1,0:T(4,128)} %bitcast.21, bf16[8,4,3,4,128]{4,3,2,1,0:T(4,128)(2,1)} %bitcast.16, f32[3,3,27]{2,1,0:T(4,128)} %bitcast.22), custom_call_target="tpu_custom_call" | custom-call | tf_op jit(solution)/shard_map/scale/pallas_call | solution.py:320
  1.0 3.1 %collective-permute-start = (bf16[8,48,128]{2,1,0:T(8,128)(2,1)S(1)}, bf16[8,48,128]{2,1,0:T(8,128)(2,1)S(1)}, u32[]{:S(2)}, u32[]{:S(2)}) collective-permute-start(bf16[8,48,128]{2,1,0:T(8,128)(2,1)S(1)} %get-tuple-element.9.refs_0_), channel_id=1, source_target_pairs={{0,1},{1,0},{2,3},{3,2},{4,5},{5,4},{6,7},{7,6},{8,9},{9,8},{10,11... | collective-permute-start | bytes 294920 | tf_op jit(solution)/shard_map/ppermute | solution.py:266
  4.1 0.0 collective-permute-start.1
  4.1 2.0 %collective-permute-start.2 = (bf16[8,12,128]{2,1,0:T(8,128)(2,1)S(1)}, bf16[8,12,128]{2,1,0:T(8,128)(2,1)S(1)}, u32[]{:S(2)}, u32[]{:S(2)}) collective-permute-start(bf16[8,12,128]{2,1,0:T(8,128)(2,1)S(1)} %get-tuple-element.18), channel_id=1, source_target_pairs={{0,2},{2,4},{4,6},{6,14},{8,0},{10,8},{12,10},{14,12},{16,18},{18,... | collective-permute-start | bytes 73736 | tf_op jit(solution)/shard_map/ppermute | solution.py:294
  6.1 2.1 %collective-permute-done.1 = bf16[8,12,128]{2,1,0:T(8,128)(2,1)S(1)} collective-permute-done((bf16[8,12,128]{2,1,0:T(8,128)(2,1)S(1)}, bf16[8,12,128]{2,1,0:T(8,128)(2,1)S(1)}, u32[]{:S(2)}, u32[]{:S(2)}) %collective-permute-start.1) | collective-permute-done | bytes 24608 | tf_op jit(solution)/shard_map/ppermute | solution.py:295
  8.2 0.0 collective-permute-done.2
  8.3 0.1 collective-permute-start.3
  8.4 4.1 %collective-permute-done.3.refs_3_ = bf16[8,24,128]{2,1,0:T(8,128)(2,1)S(1)} collective-permute-done((bf16[8,24,128]{2,1,0:T(8,128)(2,1)S(1)}, bf16[8,24,128]{2,1,0:T(8,128)(2,1)S(1)}, u32[]{:S(2)}, u32[]{:S(2)}) %collective-permute-start.3) | collective-permute-done | bytes 49184 | tf_op jit(solution)/shard_map/ppermute | solution.py:266
  12.4 0.0 collective-permute-done.refs_1_
  12.5 0.1 collective-permute-start.4
  12.6 1.6 %collective-permute-start.6 = (bf16[72,128]{1,0:T(8,128)(2,1)S(1)}, bf16[72,128]{1,0:T(8,128)(2,1)S(1)}, u32[]{:S(2)}, u32[]{:S(2)}) collective-permute-start(bf16[72,128]{1,0:T(8,128)(2,1)S(1)} %maximum_select_fusion.2), channel_id=1, source_target_pairs={{0,25},{1,24},{8,17},{9,16},{16,9},{17,8},{24,1},{25,0},{2,27},{3,... | collective-permute-start | bytes 55304 | tf_op jit(solution)/shard_map/ppermute | solution.py:230
  14.2 0.1 collective-permute-start.5
  14.3 0.5 %weights.1.weights_ref = bf16[9,96,128]{2,1,0:T(8,128)(2,1)S(1)} custom-call(f32[3,3,27]{2,1,0:T(4,128)S(1)} %get-tuple-element.8.stencil_ref), custom_call_target="tpu_custom_call" | custom-call | tf_op jit(solution)/shard_map/weights/pallas_call | solution.py:338
  14.9 0.8 %image.1.tiles_ref = bf16[4,10,192,128]{3,2,1,0:T(8,128)(2,1)S(1)} custom-call(bf16[9,96,128]{2,1,0:T(8,128)(2,1)S(1)} %weights.1.weights_ref, bf16[8,48,128]{2,1,0:T(8,128)(2,1)S(1)} %get-tuple-element.9.refs_0_, bf16[8,48,128]{2,1,0:T(8,128)(2,1)S(1)} %collective-permute-done.refs_1_), custom_call_target="tpu_custom_call" | custom-call | tf_op jit(solution)/shard_map/image/pallas_call | solution.py:360
  15.7 0.6 %middle.1.refs_2_ = f32[3456,128]{1,0:T(8,128)S(1)} custom-call(bf16[4,10,192,128]{3,2,1,0:T(8,128)(2,1)S(1)} %image.1.tiles_ref, bf16[8,48,128]{2,1,0:T(8,128)(2,1)S(1)} %get-tuple-element.9.refs_0_, bf16[8,48,128]{2,1,0:T(8,128)(2,1)S(1)} %collective-permute-done.refs_1_, bf16[8,24,128]{2,1,0:T(8,128)(2,1)S(1)} %pad_maximum_fusion.refs_2_, ...), custom_call_target="tpu_custom_call" | custom-call | tf_op jit(solution)/shard_map/middle/pallas_call | solution.py:373
  16.3 0.5 %collective-permute-done.6 = bf16[72,128]{1,0:T(8,128)(2,1)S(1)} collective-permute-done((bf16[72,128]{1,0:T(8,128)(2,1)S(1)}, bf16[72,128]{1,0:T(8,128)(2,1)S(1)}, u32[]{:S(2)}, u32[]{:S(2)}) %collective-permute-start.6) | collective-permute-done | bytes 18464 | tf_op jit(solution)/shard_map/ppermute | solution.py:230
  16.7 0.6 %collective-permute-done.5 = bf16[72,128]{1,0:T(8,128)(2,1)S(1)} collective-permute-done((bf16[72,128]{1,0:T(8,128)(2,1)S(1)}, bf16[72,128]{1,0:T(8,128)(2,1)S(1)}, u32[]{:S(2)}, u32[]{:S(2)}) %collective-permute-start.5) | collective-permute-done | bytes 18464 | tf_op jit(solution)/shard_map/ppermute | solution.py:230
  17.4 0.0 collective-permute-done.4
  17.4 1.4 %final.1 = (f32[3456,128]{1,0:T(8,128)S(1)}, f32[3456,128]{1,0:T(8,128)}) custom-call(bf16[4,10,192,128]{3,2,1,0:T(8,128)(2,1)S(1)} %image.1.tiles_ref, bf16[2,72,128]{2,1,0:T(8,128)(2,1)S(1)} %pad_maximum_fusion.3.refs_0_, bf16[2,72,128]{2,1,0:T(8,128)(2,1)S(1)} %pad_maximum_fusion.4.refs_1_, ...), custom_call_target="tpu_custom_call", output_to_operand_aliasing={{0}: (3, {})} | custom-call | tf_op jit(solution)/shard_map/final/pallas_call | solution.py:381
  (15 shorter events, 0.1 us)
Async XLA Ops:
  1.0 11.4 %collective-permute-start = (bf16[8,48,128]{2,1,0:T(8,128)(2,1)S(1)}, bf16[8,48,128]{2,1,0:T(8,128)(2,1)S(1)}, u32[]{:S(2)}, u32[]{:S(2)}) collective-permute-start(bf16[8,48,128]{2,1,0:T(8,128)(2,1)S(1)} %get-tuple-element.9.refs_0_), channel_id=1, source_target_pairs={{0,1},{1,0},{2,3},{3,2},{4,5},{5,4},{6,7},{7,6},{8,9},{9,8},{10,11... | collective-permute-start | bytes 294920 | tf_op jit(solution)/shard_map/ppermute | solution.py:266
  4.1 4.2 %collective-permute-start.1 = (bf16[8,12,128]{2,1,0:T(8,128)(2,1)S(1)}, bf16[8,12,128]{2,1,0:T(8,128)(2,1)S(1)}, u32[]{:S(2)}, u32[]{:S(2)}) collective-permute-start(bf16[8,12,128]{2,1,0:T(8,128)(2,1)S(1)} %get-tuple-element.17), channel_id=1, source_target_pairs={{2,0},{4,2},{6,4},{14,6},{0,8},{8,10},{10,12},{12,14},{18,16},{20,... | collective-permute-start | bytes 73736 | tf_op jit(solution)/shard_map/ppermute | solution.py:295
  4.1 4.1 %collective-permute-start.2 = (bf16[8,12,128]{2,1,0:T(8,128)(2,1)S(1)}, bf16[8,12,128]{2,1,0:T(8,128)(2,1)S(1)}, u32[]{:S(2)}, u32[]{:S(2)}) collective-permute-start(bf16[8,12,128]{2,1,0:T(8,128)(2,1)S(1)} %get-tuple-element.18), channel_id=1, source_target_pairs={{0,2},{2,4},{4,6},{6,14},{8,0},{10,8},{12,10},{14,12},{16,18},{18,... | collective-permute-start | bytes 73736 | tf_op jit(solution)/shard_map/ppermute | solution.py:294
  8.3 4.2 %collective-permute-start.3 = (bf16[8,24,128]{2,1,0:T(8,128)(2,1)S(1)}, bf16[8,24,128]{2,1,0:T(8,128)(2,1)S(1)}, u32[]{:S(2)}, u32[]{:S(2)}) collective-permute-start(bf16[8,24,128]{2,1,0:T(8,128)(2,1)S(1)} %pad_maximum_fusion.refs_2_), channel_id=1, source_target_pairs={{0,1},{1,0},{2,3},{3,2},{4,5},{5,4},{6,7},{7,6},{8,9},{9,8},{10,11... | collective-permute-start | bytes 147464 | tf_op jit(solution)/shard_map/ppermute | solution.py:266
  12.5 4.9 %collective-permute-start.4 = (bf16[2,72,128]{2,1,0:T(8,128)(2,1)S(1)}, bf16[2,72,128]{2,1,0:T(8,128)(2,1)S(1)}, u32[]{:S(2)}, u32[]{:S(2)}) collective-permute-start(bf16[2,72,128]{2,1,0:T(8,128)(2,1)S(1)} %pad_maximum_fusion.1), channel_id=1, source_target_pairs={{0,8},{8,0},{16,24},{24,16},{1,9},{9,1},{17,25},{25,17},{2,10},{10... | collective-permute-start | bytes 110600 | tf_op jit(solution)/shard_map/ppermute | solution.py:230
  12.6 4.2 %collective-permute-start.6 = (bf16[72,128]{1,0:T(8,128)(2,1)S(1)}, bf16[72,128]{1,0:T(8,128)(2,1)S(1)}, u32[]{:S(2)}, u32[]{:S(2)}) collective-permute-start(bf16[72,128]{1,0:T(8,128)(2,1)S(1)} %maximum_select_fusion.2), channel_id=1, source_target_pairs={{0,25},{1,24},{8,17},{9,16},{16,9},{17,8},{24,1},{25,0},{2,27},{3,... | collective-permute-start | bytes 55304 | tf_op jit(solution)/shard_map/ppermute | solution.py:230
  14.2 3.2 %collective-permute-start.5 = (bf16[72,128]{1,0:T(8,128)(2,1)S(1)}, bf16[72,128]{1,0:T(8,128)(2,1)S(1)}, u32[]{:S(2)}, u32[]{:S(2)}) collective-permute-start(bf16[72,128]{1,0:T(8,128)(2,1)S(1)} %maximum_select_fusion.2), channel_id=1, source_target_pairs={{0,24},{8,16},{16,8},{24,0},{1,25},{9,17},{17,9},{25,1},{2,26},{10... | collective-permute-start | bytes 55304 | tf_op jit(solution)/shard_map/ppermute | solution.py:230

commit v2 on v1

--- a/solution.py
+++ b/solution.py
@@ -199,8 +199,20 @@
             put(9 + 3 * oy + oz, place[u], total[oy * share : (oy + 1) * share, :])
 
 
-def final_kernel(share, places, late, tiles_ref, *refs):
-    faces, (_, whole_ref, out_ref, sem) = refs[: len(late)], refs[len(late) :]
+def final_kernel(share, places, late, wide, tiles_ref, *refs):
+    pieces, (_, whole_ref, out_ref, sem) = refs[:-4], refs[-4:]
+    if len(pieces) == len(late):
+        faces = dict(zip(late, pieces))
+    else:
+        beside, *across = pieces
+        column = lax.axis_index("gx")
+        odd = column % 2 == 1
+        faces = {}
+        for v in late:
+            near, far = beside[v], across[v][...]
+            zero = jnp.zeros_like(near)
+            left, right = jnp.where(odd, near, far), jnp.where(odd, far, near)
+            faces[v] = [jnp.where(column == 0, zero, left), jnp.where(column == wide - 1, zero, right)]
     owners = len(places(0))
     place = places(lax.axis_index("gz"))
     rounds = sem.shape[0]
@@ -209,7 +221,7 @@
     for i in range(rounds):
         put = putter(size, owners, whole_ref, i * size)
         for pair, (u, v, oz) in enumerate(pairs_of(owners, place)):
-            sides(share, put, tiles_ref, pair, place[u], oz, faces[late.index(v)], i * size, size)
+            sides(share, put, tiles_ref, pair, place[u], oz, faces[v], i * size, size)
         span = pl.ds(i * size * 27 * owners, size * 27 * owners)
         copies.append(pltpu.make_async_copy(whole_ref.at[span], out_ref.at[span], sem.at[i]))
         copies[-1].start()
@@ -250,10 +262,7 @@
         next_to = exchange(across, ("gx",), False, 1)
         beside = jnp.stack([jnp.where(odd, edge(v, 0), edge(v, cells_x - 1)) for v in range(owners)])
         beside = exchange(beside, ("gx",), False, 0)
-        across = jnp.stack([next_to, far])
-        left, right = jnp.where(odd, beside, across), jnp.where(odd, across, beside)
-        zero = jnp.zeros_like(left)
-        left, right = jnp.where(place == 0, zero, left), jnp.where(place == wide - 1, zero, right)
+        return [beside, next_to, far]
     return [jnp.stack([left[v], right[v]]) for v in range(owners)]
 
 
@@ -379,15 +388,15 @@
         name="middle",
     )(tiles, *cells, *rims, *(faces[v] for v in early))
     _, coarse = pl.pallas_call(
-        functools.partial(final_kernel, share, places, late),
+        functools.partial(final_kernel, share, places, late, lax.axis_size("gx")),
         out_shape=(pltpu.VMEM(whole.shape, whole.dtype), whole),
-        in_specs=[in_vmem] * (2 + len(late)),
+        in_specs=[in_vmem] * (2 + len(faces)),
         out_specs=(in_vmem, pl.BlockSpec(memory_space=pltpu.HBM)),
         scratch_shapes=[pltpu.SemaphoreType.DMA((ROUNDS,))],
-        input_output_aliases={1 + len(late): 0},
+        input_output_aliases={1 + len(faces): 0},
         compiler_params=small,
         name="final",
-    )(tiles, *(faces[v] for v in late), coarse)
+    )(tiles, *faces, coarse)
     coarse = coarse.reshape(share, 27, owners, width)
     return jnp.transpose(coarse, (0, 2, 1, 3)).reshape(1, 1, share, owners, 27, width)
 

time: 19 us -> 19 us (level)
  no operation moved by 1% of the time
where the time goes in v2:
time: 19 us; the launch traced here: 18.8 us
  waiting for transfers between devices  7.28 us (38%)
  starting transfers between devices  6.97 us (37%)
  Pallas kernels  4.33 us (23%)
    ppermute x2, waiting for transfers between devices, cyclic(): lax.ppermute(array, axis, [(i, (i + step) % peers) for i in range(peers)])  4.06 us
    ppermute x2, starting transfers between devices, cyclic(): lax.ppermute(array, axis, [(i, (i + step) % peers) for i in range(peers)])  3.13 us
    ppermute x1, waiting for transfers between devices, columns(): lax.ppermute(jnp.where(odd, last, first), ('gx', 'gy'), [(t, f) for f, t...  2.11 us
    ppermute x1, starting transfers between devices, columns(): ahead = lax.ppermute(jnp.where(odd, first, last), ('gx', 'gy'), pairs)  2.01 us
    ppermute x3, starting transfers between devices, exchange(): return lax.ppermute(array, axes, pairs)  1.8 us
    pallas_call x1, Pallas kernels, blocks(): pl.pallas_call(functools.partial(final_kernel, share, places, late, lax.a...  1.43 us
    ppermute x3, waiting for transfers between devices, exchange(): return lax.ppermute(array, axes, pairs)  1.11 us
    pallas_call x1, Pallas kernels, blocks(): pl.pallas_call(scale_kernel, out_shape=(jax.ShapeDtypeStruct((cells_x, ow...  0.98 us
  transfers between devices with their start and end apart: 7, of which 4 were waited for; matrix products, arithmetic and copies ran while one was open for 0% of the time, Pallas kernels for 10%

profile of v2, /device:TPU:0, one launch (start us, length us, event | category | flops | bytes accessed | tf_op | source)
XLA Modules:
  0.0 18.8 jit_solution(8042583007284227971)
XLA Ops:
  0.0 1.0 %scale.1 = (bf16[8,48,128]{2,1,0:T(8,128)(2,1)S(1)}, f32[3,3,27]{2,1,0:T(4,128)S(1)}) custom-call(f32[16]{0:T(128)} %moduli_hbm.1, s32[4,4,8]{2,1,0:T(4,128)} %bitcast.17, bf16[8,4,3,4,128]{4,3,2,1,0:T(4,128)(2,1)} %bitcast.14, f32[3,3,27]{2,1,0:T(4,128)} %bitcast.18), custom_call_target="tpu_custom_call" | custom-call | tf_op jit(solution)/shard_map/scale/pallas_call | solution.py:329
  1.0 3.1 %collective-permute-start = (bf16[8,48,128]{2,1,0:T(8,128)(2,1)S(1)}, bf16[8,48,128]{2,1,0:T(8,128)(2,1)S(1)}, u32[]{:S(2)}, u32[]{:S(2)}) collective-permute-start(bf16[8,48,128]{2,1,0:T(8,128)(2,1)S(1)} %get-tuple-element.9.refs_0_), channel_id=1, source_target_pairs={{0,1},{1,0},{2,3},{3,2},{4,5},{5,4},{6,7},{7,6},{8,9},{9,8},{10,11... | collective-permute-start | bytes 294920 | tf_op jit(solution)/shard_map/ppermute | solution.py:275
  4.1 0.0 collective-permute-start.1
  4.1 2.0 %collective-permute-start.2 = (bf16[8,12,128]{2,1,0:T(8,128)(2,1)S(1)}, bf16[8,12,128]{2,1,0:T(8,128)(2,1)S(1)}, u32[]{:S(2)}, u32[]{:S(2)}) collective-permute-start(bf16[8,12,128]{2,1,0:T(8,128)(2,1)S(1)} %get-tuple-element.18), channel_id=1, source_target_pairs={{0,2},{2,4},{4,6},{6,14},{8,0},{10,8},{12,10},{14,12},{16,18},{18,... | collective-permute-start | bytes 73736 | tf_op jit(solution)/shard_map/ppermute | solution.py:303
  6.1 2.1 %collective-permute-done.1 = bf16[8,12,128]{2,1,0:T(8,128)(2,1)S(1)} collective-permute-done((bf16[8,12,128]{2,1,0:T(8,128)(2,1)S(1)}, bf16[8,12,128]{2,1,0:T(8,128)(2,1)S(1)}, u32[]{:S(2)}, u32[]{:S(2)}) %collective-permute-start.1) | collective-permute-done | bytes 24608 | tf_op jit(solution)/shard_map/ppermute | solution.py:304
  8.2 0.0 collective-permute-done.2
  8.3 0.1 collective-permute-start.3
  8.4 4.1 %collective-permute-done.3.refs_3_ = bf16[8,24,128]{2,1,0:T(8,128)(2,1)S(1)} collective-permute-done((bf16[8,24,128]{2,1,0:T(8,128)(2,1)S(1)}, bf16[8,24,128]{2,1,0:T(8,128)(2,1)S(1)}, u32[]{:S(2)}, u32[]{:S(2)}) %collective-permute-start.3) | collective-permute-done | bytes 49184 | tf_op jit(solution)/shard_map/ppermute | solution.py:275
  12.4 0.0 collective-permute-done.refs_1_
  12.5 0.1 collective-permute-start.4
  12.6 1.6 %collective-permute-start.6 = (bf16[72,128]{1,0:T(8,128)(2,1)S(1)}, bf16[72,128]{1,0:T(8,128)(2,1)S(1)}, u32[]{:S(2)}, u32[]{:S(2)}) collective-permute-start(bf16[72,128]{1,0:T(8,128)(2,1)S(1)} %maximum_select_fusion.2), channel_id=1, source_target_pairs={{0,25},{1,24},{8,17},{9,16},{16,9},{17,8},{24,1},{25,0},{2,27},{3,... | collective-permute-start | bytes 55304 | tf_op jit(solution)/shard_map/ppermute | solution.py:242
  14.2 0.1 collective-permute-start.5
  14.3 0.5 %weights.1.weights_ref = bf16[9,96,128]{2,1,0:T(8,128)(2,1)S(1)} custom-call(f32[3,3,27]{2,1,0:T(4,128)S(1)} %get-tuple-element.8.stencil_ref), custom_call_target="tpu_custom_call" | custom-call | tf_op jit(solution)/shard_map/weights/pallas_call | solution.py:347
  14.9 0.8 %image.1.tiles_ref = bf16[4,10,192,128]{3,2,1,0:T(8,128)(2,1)S(1)} custom-call(bf16[9,96,128]{2,1,0:T(8,128)(2,1)S(1)} %weights.1.weights_ref, bf16[8,48,128]{2,1,0:T(8,128)(2,1)S(1)} %get-tuple-element.9.refs_0_, bf16[8,48,128]{2,1,0:T(8,128)(2,1)S(1)} %collective-permute-done.refs_1_), custom_call_target="tpu_custom_call" | custom-call | tf_op jit(solution)/shard_map/image/pallas_call | solution.py:369
  15.7 0.6 %middle.1.refs_3_ = f32[3456,128]{1,0:T(8,128)S(1)} custom-call(bf16[4,10,192,128]{3,2,1,0:T(8,128)(2,1)S(1)} %image.1.tiles_ref, bf16[8,48,128]{2,1,0:T(8,128)(2,1)S(1)} %get-tuple-element.9.refs_0_, bf16[8,48,128]{2,1,0:T(8,128)(2,1)S(1)} %collective-permute-done.refs_1_, bf16[8,24,128]{2,1,0:T(8,128)(2,1)S(1)} %pad_maximum_fusion.refs_2_, ...), custom_call_target="tpu_custom_call" | custom-call | tf_op jit(solution)/shard_map/middle/pallas_call | solution.py:382
  16.3 0.5 %collective-permute-done.6.refs_2_ = bf16[72,128]{1,0:T(8,128)(2,1)S(1)} collective-permute-done((bf16[72,128]{1,0:T(8,128)(2,1)S(1)}, bf16[72,128]{1,0:T(8,128)(2,1)S(1)}, u32[]{:S(2)}, u32[]{:S(2)}) %collective-permute-start.6) | collective-permute-done | bytes 18464 | tf_op jit(solution)/shard_map/ppermute | solution.py:242
  16.7 0.6 %collective-permute-done.5.refs_1_ = bf16[72,128]{1,0:T(8,128)(2,1)S(1)} collective-permute-done((bf16[72,128]{1,0:T(8,128)(2,1)S(1)}, bf16[72,128]{1,0:T(8,128)(2,1)S(1)}, u32[]{:S(2)}, u32[]{:S(2)}) %collective-permute-start.5) | collective-permute-done | bytes 18464 | tf_op jit(solution)/shard_map/ppermute | solution.py:242
  17.4 0.0 collective-permute-done.4.refs_0_
  17.4 1.4 %final.1 = (f32[3456,128]{1,0:T(8,128)S(1)}, f32[3456,128]{1,0:T(8,128)}) custom-call(bf16[4,10,192,128]{3,2,1,0:T(8,128)(2,1)S(1)} %image.1.tiles_ref, bf16[2,72,128]{2,1,0:T(8,128)(2,1)S(1)} %collective-permute-done.4.refs_0_, bf16[72,128]{1,0:T(8,128)(2,1)S(1)} %collective-permute-done.5.refs_1_, ...), custom_call_target="tpu_custom_call", output_to_operand_aliasing={{0}: (4, {})} | custom-call | tf_op jit(solution)/shard_map/final/pallas_call | solution.py:390
  (10 shorter events, 0.1 us)
Async XLA Ops:
  1.0 11.4 %collective-permute-start = (bf16[8,48,128]{2,1,0:T(8,128)(2,1)S(1)}, bf16[8,48,128]{2,1,0:T(8,128)(2,1)S(1)}, u32[]{:S(2)}, u32[]{:S(2)}) collective-permute-start(bf16[8,48,128]{2,1,0:T(8,128)(2,1)S(1)} %get-tuple-element.9.refs_0_), channel_id=1, source_target_pairs={{0,1},{1,0},{2,3},{3,2},{4,5},{5,4},{6,7},{7,6},{8,9},{9,8},{10,11... | collective-permute-start | bytes 294920 | tf_op jit(solution)/shard_map/ppermute | solution.py:275
  4.1 4.2 %collective-permute-start.1 = (bf16[8,12,128]{2,1,0:T(8,128)(2,1)S(1)}, bf16[8,12,128]{2,1,0:T(8,128)(2,1)S(1)}, u32[]{:S(2)}, u32[]{:S(2)}) collective-permute-start(bf16[8,12,128]{2,1,0:T(8,128)(2,1)S(1)} %get-tuple-element.17), channel_id=1, source_target_pairs={{2,0},{4,2},{6,4},{14,6},{0,8},{8,10},{10,12},{12,14},{18,16},{20,... | collective-permute-start | bytes 73736 | tf_op jit(solution)/shard_map/ppermute | solution.py:304
  4.1 4.1 %collective-permute-start.2 = (bf16[8,12,128]{2,1,0:T(8,128)(2,1)S(1)}, bf16[8,12,128]{2,1,0:T(8,128)(2,1)S(1)}, u32[]{:S(2)}, u32[]{:S(2)}) collective-permute-start(bf16[8,12,128]{2,1,0:T(8,128)(2,1)S(1)} %get-tuple-element.18), channel_id=1, source_target_pairs={{0,2},{2,4},{4,6},{6,14},{8,0},{10,8},{12,10},{14,12},{16,18},{18,... | collective-permute-start | bytes 73736 | tf_op jit(solution)/shard_map/ppermute | solution.py:303
  8.3 4.2 %collective-permute-start.3 = (bf16[8,24,128]{2,1,0:T(8,128)(2,1)S(1)}, bf16[8,24,128]{2,1,0:T(8,128)(2,1)S(1)}, u32[]{:S(2)}, u32[]{:S(2)}) collective-permute-start(bf16[8,24,128]{2,1,0:T(8,128)(2,1)S(1)} %pad_maximum_fusion.refs_2_), channel_id=1, source_target_pairs={{0,1},{1,0},{2,3},{3,2},{4,5},{5,4},{6,7},{7,6},{8,9},{9,8},{10,11... | collective-permute-start | bytes 147464 | tf_op jit(solution)/shard_map/ppermute | solution.py:275
  12.5 4.9 %collective-permute-start.4 = (bf16[2,72,128]{2,1,0:T(8,128)(2,1)S(1)}, bf16[2,72,128]{2,1,0:T(8,128)(2,1)S(1)}, u32[]{:S(2)}, u32[]{:S(2)}) collective-permute-start(bf16[2,72,128]{2,1,0:T(8,128)(2,1)S(1)} %pad_maximum_fusion.1), channel_id=1, source_target_pairs={{0,8},{8,0},{16,24},{24,16},{1,9},{9,1},{17,25},{25,17},{2,10},{10... | collective-permute-start | bytes 110600 | tf_op jit(solution)/shard_map/ppermute | solution.py:242
  12.6 4.2 %collective-permute-start.6 = (bf16[72,128]{1,0:T(8,128)(2,1)S(1)}, bf16[72,128]{1,0:T(8,128)(2,1)S(1)}, u32[]{:S(2)}, u32[]{:S(2)}) collective-permute-start(bf16[72,128]{1,0:T(8,128)(2,1)S(1)} %maximum_select_fusion.2), channel_id=1, source_target_pairs={{0,25},{1,24},{8,17},{9,16},{16,9},{17,8},{24,1},{25,0},{2,27},{3,... | collective-permute-start | bytes 55304 | tf_op jit(solution)/shard_map/ppermute | solution.py:242
  14.2 3.2 %collective-permute-start.5 = (bf16[72,128]{1,0:T(8,128)(2,1)S(1)}, bf16[72,128]{1,0:T(8,128)(2,1)S(1)}, u32[]{:S(2)}, u32[]{:S(2)}) collective-permute-start(bf16[72,128]{1,0:T(8,128)(2,1)S(1)} %maximum_select_fusion.2), channel_id=1, source_target_pairs={{0,24},{8,16},{16,8},{24,0},{1,25},{9,17},{17,9},{25,1},{2,26},{10... | collective-permute-start | bytes 55304 | tf_op jit(solution)/shard_map/ppermute | solution.py:242
